TPU v7x, 32 devices: a whole 2x2x4 slice. The times are simulated.
32 devices in a mesh: gx: 8 (over z, y), gy: 4 (over x, core).
Axes of the slice: x: 2, y: 2, z: 4, core: 2. Of those that a mesh axis runs over, the one named last changes fastest.
Arguments:
- table: float32 [4, 65536, 128], P(None, 'gx'), may hold values from -2.1 to 2.1
- lookup_owner: int32 [4, 8192, 16, 1], P(None, ('gx', 'gy')), may hold values from 0 to 7; in each aligned block of 4096 rows (0 to 4095, 4096 to 8191, ..., all dimensions but the last counted through in order) at most 1024 rows name the same one
- lookup_row: int32 [4, 8192, 16], P(None, ('gx', 'gy')), may hold values from 0 to 8191
- bag_length: int32 [4, 8192], P(None, ('gx', 'gy')), may hold values from 1 to 16
- top_in: bfloat16 [512, 8192], P(None, 'gy'), may hold values from -0.25 to 0.25
- top_bias: float32 [8192], P('gy'), may hold values from -3 to 3
- top_out: bfloat16 [8192, 1024], P('gy'), may hold values from -0.0625 to 0.0625
Outputs:
- scored: bfloat16 [8192, 1024], P(('gx', 'gy'))
Inputs may be any that keep to these rules, and one draw needn't show every extreme that they name: `lookup_owner`: in every aligned block of 4096 entries (the lookups of one table from the samples of one device) no owner is named more than 1024 times; some blocks reach 1024.
All inputs are finite; a program needn't handle non-finite values.
Results may differ from a plain program's by a relative error of at most 0.0057.
Values may be sent and summed in bfloat16 or wider, within the bound.
A program may use at most 128 MiB of HBM per device.

v0:
```python
import jax
import jax.numpy as jnp
from jax import lax
from jax.sharding import PartitionSpec as P


def local(table, lookup_owner, lookup_row, bag_length, top_in, top_bias, top_out):
    owners = lax.axis_size("gx")
    tables, samples, bag_size = lookup_row.shape
    rows_dev = table.shape[1]
    emb_width = table.shape[2]
    slot_count = 2 * samples * bag_size // owners
    lookups = samples * bag_size
    owner_of = lookup_owner[..., 0].reshape(tables, lookups)
    local_row = lookup_row.reshape(tables, lookups)
    is_live = jnp.arange(bag_size, dtype=jnp.int32)[None, None, :] < bag_length[:, :, None]
    sample_ids = jnp.broadcast_to(
        jnp.arange(samples, dtype=jnp.int32)[None, :, None], (tables, samples, bag_size)
    )
    bag_codes = jnp.where(is_live, sample_ids, samples).reshape(tables, lookups)
    onehot = (owner_of[:, :, None] == jnp.arange(owners, dtype=jnp.int32)[None, None, :]).astype(
        jnp.int32
    )
    slot_rank = jnp.sum((jnp.cumsum(onehot, axis=1) - onehot) * onehot, axis=2)
    table_ids = jnp.broadcast_to(jnp.arange(tables, dtype=jnp.int32)[:, None], (tables, lookups))
    flat_row = local_row + table_ids * rows_dev
    destination = owner_of * slot_count + slot_rank
    carried = jnp.stack(
        [
            flat_row // 256,
            flat_row % 256,
            bag_codes // 256,
            bag_codes % 256,
            jnp.ones_like(flat_row),
        ],
        axis=2,
    ).astype(jnp.bfloat16)
    slot_iota = jnp.arange(slot_count, dtype=jnp.int32)

    def fill_table(pieces):
        dest_one, carried_one = pieces

        def fill_owner(owner_id):
            marks = (dest_one[None, :] == owner_id * slot_count + slot_iota[:, None]).astype(
                jnp.bfloat16
            )
            return jnp.dot(marks, carried_one, preferred_element_type=jnp.float32)

        return lax.map(fill_owner, jnp.arange(owners, dtype=jnp.int32))

    filled = lax.map(fill_table, (destination, carried))
    filled = jnp.transpose(filled, (1, 0, 2, 3))
    sent_rows = (filled[..., 0] * 256.0 + filled[..., 1]).astype(jnp.int32)
    sent_codes = (
        filled[..., 2] * 256.0 + filled[..., 3] + (1.0 - filled[..., 4]) * samples
    ).astype(jnp.int32)
    flat_table = table.reshape(tables * rows_dev, emb_width)

    def pool_source(pieces):
        codes_one, rows_one = pieces
        selector = (
            codes_one[:, None, :] == jnp.arange(samples, dtype=jnp.int32)[None, :, None]
        ).astype(jnp.float32)
        return jnp.einsum(
            "tbs,tsd->tbd",
            selector,
            rows_one,
            precision=lax.Precision.HIGHEST,
            preferred_element_type=jnp.float32,
        )

    rows_in = lax.all_to_all(sent_rows, "gx", split_axis=0, concat_axis=0, tiled=True)
    codes_in = lax.all_to_all(sent_codes, "gx", split_axis=0, concat_axis=0, tiled=True)
    gathered = jnp.take(flat_table, rows_in, axis=0)
    partial_value = lax.map(pool_source, (codes_in, gathered))
    answer = lax.all_to_all(partial_value, "gx", split_axis=0, concat_axis=0, tiled=True)
    pooled = jnp.sum(answer, axis=0)
    features = (
        jnp.transpose(pooled, (1, 0, 2)).reshape(samples, tables * emb_width).astype(jnp.bfloat16)
    )
    pre_act = (
        jnp.dot(
            lax.all_gather(features, "gy", axis=0, tiled=True),
            top_in,
            preferred_element_type=jnp.float32,
        )
        + top_bias
    )
    hidden_rows = jnp.maximum(pre_act, 0.0).astype(jnp.bfloat16)
    scored = lax.psum_scatter(
        jnp.dot(hidden_rows, top_out, preferred_element_type=jnp.float32),
        "gy",
        scatter_dimension=0,
        tiled=True,
    )
    return scored.astype(jnp.bfloat16)


def solution(mesh):
    return jax.shard_map(
        local,
        mesh=mesh,
        in_specs=(
            P(None, "gx", None),
            P(None, ("gx", "gy"), None, None),
            P(None, ("gx", "gy"), None),
            P(None, ("gx", "gy")),
            P(None, "gy"),
            P("gy"),
            P("gy", None),
        ),
        out_specs=P(("gx", "gy"), None),
        check_vma=False,
    )
```

profile of v0, /device:TPU:0, one launch (start us, length us, event | category | flops | bytes accessed | tf_op | source)
XLA Modules:
  0.0 526.4 jit_solution(17502736940000704099)
XLA Ops:
  8.3 9.2 %reduce-window.6 = s32[4,8,32,128]{3,2,1,0:T(8,128)S(1)} reduce-window(s32[4,8,32,128]{3,2,1,0:T(8,128)S(1)} %fusion.30, s32[]{:T(128)} %copy.57), window={size=1x1x1x128 pad=0_0x0_0x0_0x127_0}, to_apply=%region_0.1 | reduce-window | flops 16646144 | bytes 1048580 | tf_op jit(solution)/shard_map/reduce-window
  26.4 135.1 %while.34 = (s32[]{:T(128)}, f32[4,8,1024,5]{2,0,1,3:T(4,128)S(1)}, s32[4,4096]{1,0:T(4,128)}, bf16[4,4096,5]{1,2,0:T(8,128)(2,1)S(1)}, s32[]{:T(128)}, /*index=5*/s32[]{:T(128)}, s32[]{:T(128)}, s32[1]{0:T(128)}) while((s32[]{:T(128)}, f32[4,8,1024,5]{2,0,1,3:T(4,128)S(1)}, s32[4,4096]{1,0:T(4,128)}, ...), condition=%wide.region_6.7_spmd.clone, body=%wide.region_3.6_spmd.clone.sunk | while | flops 46138368 | bytes 901438 | solution.py:51
  27.4 31.4 %while.35 = (s32[]{:T(128)}, f32[8,1024,5]{1,2,0:T(8,128)S(1)}, s32[4096]{0:T(1024)S(1)}, s32[8]{0:T(128)S(1)}, s32[1024]{0:T(1024)S(1)}, /*index=5*/bf16[4096,5]{0,1:T(8,128)(2,1)S(1)}, s32[]{:T(128)}, s32[1]{0:T(128)}) while((s32[]{:T(128)}, f32[8,1024,5]{1,2,0:T(8,128)S(1)}, s32[4096]{0:T(1024)S(1)}, s32[8]{0:T(128)S(1)}, ...), condition=%wide.region_5.5_spmd, body=%wide.region_4.4_spmd.sunk | while | flops 46138368 | bytes 127093 | solution.py:49
  61.1 31.4 %while.35 = (s32[]{:T(128)}, f32[8,1024,5]{1,2,0:T(8,128)S(1)}, s32[4096]{0:T(1024)S(1)}, s32[8]{0:T(128)S(1)}, s32[1024]{0:T(1024)S(1)}, /*index=5*/bf16[4096,5]{0,1:T(8,128)(2,1)S(1)}, s32[]{:T(128)}, s32[1]{0:T(128)}) while((s32[]{:T(128)}, f32[8,1024,5]{1,2,0:T(8,128)S(1)}, s32[4096]{0:T(1024)S(1)}, s32[8]{0:T(128)S(1)}, ...), condition=%wide.region_5.5_spmd, body=%wide.region_4.4_spmd.sunk | while | flops 46138368 | bytes 127093 | solution.py:49
  94.9 31.4 %while.35 = (s32[]{:T(128)}, f32[8,1024,5]{1,2,0:T(8,128)S(1)}, s32[4096]{0:T(1024)S(1)}, s32[8]{0:T(128)S(1)}, s32[1024]{0:T(1024)S(1)}, /*index=5*/bf16[4096,5]{0,1:T(8,128)(2,1)S(1)}, s32[]{:T(128)}, s32[1]{0:T(128)}) while((s32[]{:T(128)}, f32[8,1024,5]{1,2,0:T(8,128)S(1)}, s32[4096]{0:T(1024)S(1)}, s32[8]{0:T(128)S(1)}, ...), condition=%wide.region_5.5_spmd, body=%wide.region_4.4_spmd.sunk | while | flops 46138368 | bytes 127093 | solution.py:49
  128.7 31.4 %while.35 = (s32[]{:T(128)}, f32[8,1024,5]{1,2,0:T(8,128)S(1)}, s32[4096]{0:T(1024)S(1)}, s32[8]{0:T(128)S(1)}, s32[1024]{0:T(1024)S(1)}, /*index=5*/bf16[4096,5]{0,1:T(8,128)(2,1)S(1)}, s32[]{:T(128)}, s32[1]{0:T(128)}) while((s32[]{:T(128)}, f32[8,1024,5]{1,2,0:T(8,128)S(1)}, s32[4096]{0:T(1024)S(1)}, s32[8]{0:T(128)S(1)}, ...), condition=%wide.region_5.5_spmd, body=%wide.region_4.4_spmd.sunk | while | flops 46138368 | bytes 127093 | solution.py:49
  162.4 7.3 %all-to-all-start.1 = ((s32[8,4,1024]{2,1,0:T(4,128)}), s32[8,4,1024]{2,1,0:T(4,128)S(1)}, u32[]{:S(2)}, u32[]{:S(2)}) async-start(s32[8,4,1024]{2,1,0:T(4,128)} %get-tuple-element.145), calls=%async_computation.1 | async-start | bytes 262144 | tf_op jit(solution)/shard_map/all_to_all | solution.py:72
  169.7 7.3 %all-to-all-done.1 = s32[8,4,1024]{2,1,0:T(4,128)S(1)} async-done(((s32[8,4,1024]{2,1,0:T(4,128)}), s32[8,4,1024]{2,1,0:T(4,128)S(1)}, u32[]{:S(2)}, u32[]{:S(2)}) %all-to-all-start.1) | async-done | bytes 131104 | tf_op jit(solution)/shard_map/all_to_all | solution.py:72
  177.0 3.4 all-to-all-start
  180.5 114.8 %gather_fusion = f32[32768,128]{1,0:T(8,128)} fusion(f32[32768,128]{1,0:T(8,128)} %bitcast.75, s32[32768]{0:T(1024)S(1)} %broadcast_clamp_fusion), kind=kCustom, calls=%fused_computation | custom fusion | bytes 33685504 | tf_op jit(solution)/shard_map/jit(_take)/gather | solution.py:74
  295.4 12.0 %broadcast_select_fusion = f32[8,4,1024,128]{3,2,1,0:T(8,128)} fusion(f32[8,4,1024,128]{3,2,1,0:T(8,128)} %bitcast.76, pred[8,4,1024]{2,1,0:T(4,128)(4,1)S(1)} %compare_and_fusion), kind=kLoop, calls=%fused_computation.21 | loop fusion | flops 4194304 | bytes 33587200 | tf_op jit(solution)/shard_map/jit(_take)/select_n | solution.py:74
  307.4 37.4 %while.32 = (s32[]{:T(128)}, f32[8,4,256,128]{3,2,1,0:T(8,128)}, s32[8,4,1024]{2,1,0:T(4,128)S(1)}, f32[8,4,1024,128]{3,2,1,0:T(8,128)}, s32[]{:T(128)}) while((s32[]{:T(128)}, f32[8,4,256,128]{3,2,1,0:T(8,128)}, s32[8,4,1024]{2,1,0:T(4,128)S(1)}, f32[8,4,1024,128]{3,2,1,0:T(8,128)}, s32[]{:T(128)}) %tuple.63), condition=%wide.region_8.9_spmd, body=%wide.region_7.8_spmd.sunk | while | flops 1611661312 | bytes 2671681 | solution.py:75
  307.4 4.7 fusion.60
  312.1 4.7 fusion.60
  316.7 4.7 fusion.60
  321.4 4.7 fusion.60
  326.1 4.7 fusion.60
  330.8 4.7 fusion.60
  335.4 4.7 fusion.60
  340.1 4.7 fusion.60
  344.8 97.5 %all_to_all.15 = f32[8,4,256,128]{3,2,1,0:T(8,128)} all-to-all(f32[8,4,256,128]{3,2,1,0:T(8,128)} %get-tuple-element.87), channel_id=1, replica_groups=mesh['gx'=8,'gy'=4] {'gx'}, dimensions={0} | all-to-all | bytes 8388608 | tf_op jit(solution)/shard_map/all_to_all | solution.py:76
  445.8 15.7 %all-gather.2.cloned.1.call-done = bf16[1024,512]{0,1:T(8,128)(2,1)} async-done(((bf16[256,512]{0,1:T(8,128)(2,1)}), bf16[1024,512]{0,1:T(8,128)(2,1)}) %all-gather.2.cloned.1.call-update) | async-done | bytes 1048592 | tf_op jit(solution)/shard_map/all_gather | solution.py:83
  461.6 11.2 %fusion.23 = f32[1024,1024]{1,0:T(8,128)} fusion(bf16[2048,1024]{1,0:T(8,128)(2,1)} %param.19, f32[2048]{0:T(1024)S(1)} %copy-done.4, bf16[1024,512]{0,1:T(8,128)(2,1)} %all-gather.2.cloned.1.call-done, bf16[512,2048]{1,0:T(8,128)(2,1)S(1)} %copy-done), kind=kOutput, calls=%fused_computation.22 | convolution fusion | flops 6448742400 | bytes 11542528 | tf_op jit(solution)/shard_map/dot_general | solution.py:91
  472.7 44.8 %reduce-scatter.2.cloned.1.call-done = f32[256,1024]{1,0:T(8,128)} async-done(((f32[1024,1024]{1,0:T(8,128)}), f32[256,1024]{1,0:T(8,128)}) %reduce-scatter.2.cloned.1.call-update) | async-done | bytes 1048592 | tf_op jit(solution)/shard_map/reduce_scatter | solution.py:90
  (182 shorter events, 131.3 us)
Async XLA Ops:
  6.5 455.0 %copy-start = (bf16[512,2048]{1,0:T(8,128)(2,1)S(1)}, bf16[512,2048]{1,0:T(8,128)(2,1)}, u32[]{:S(2)}) copy-start(bf16[512,2048]{1,0:T(8,128)(2,1)} %param.17) | copy-start | bytes 6291460
  6.5 16.2 %copy-start.3 = (s32[4,256]{1,0:T(4,128)S(1)}, s32[4,256]{1,0:T(4,128)}, u32[]{:S(2)}) copy-start(s32[4,256]{1,0:T(4,128)} %param.16) | copy-start | bytes 12292
  19.4 7.0 %copy-start.1 = (f32[4,8,1024,5]{2,0,1,3:T(4,128)S(1)}, f32[4,8,1024,5]{2,0,1,3:T(4,128)}, u32[]{:S(2)}) copy-start(f32[4,8,1024,5]{2,0,1,3:T(4,128)} %custom-call.5) | copy-start | bytes 1966084
  21.9 0.7 copy-start.2
  162.4 14.7 %all-to-all-start.1 = ((s32[8,4,1024]{2,1,0:T(4,128)}), s32[8,4,1024]{2,1,0:T(4,128)S(1)}, u32[]{:S(2)}, u32[]{:S(2)}) async-start(s32[8,4,1024]{2,1,0:T(4,128)} %get-tuple-element.145), calls=%async_computation.1 | async-start | bytes 262144 | tf_op jit(solution)/shard_map/all_to_all | solution.py:72
  177.0 130.3 %all-to-all-start = ((s32[8,4,1024]{2,1,0:T(4,128)}), s32[8,4,1024]{2,1,0:T(4,128)S(1)}, u32[]{:S(2)}, u32[]{:S(2)}) async-start(s32[8,4,1024]{2,1,0:T(4,128)} %get-tuple-element.146), calls=%async_computation | async-start | bytes 262144 | tf_op jit(solution)/shard_map/all_to_all | solution.py:73
  180.4 281.2 %all-gather.2.cloned.1.call-start = ((), (), s32[]{:S(2)}) async-start(), calls=%async_computation.4 | async-start | bytes 1310720 | tf_op jit(solution)/shard_map/all_gather | solution.py:83
  442.2 19.3 %copy-start.4 = (f32[2048]{0:T(1024)S(1)}, f32[2048]{0:T(1024)}, u32[]{:S(2)}) copy-start(f32[2048]{0:T(1024)} %param.18) | copy-start | bytes 24580
  445.6 71.9 %reduce-scatter.2.cloned.1.call-start = ((), (), s32[]{:S(2)}) async-start(), calls=%async_computation.5 | async-start | bytes 5242880 | tf_op jit(solution)/shard_map/reduce_scatter | solution.py:90
Sparse Core Ops, SparseCore 0:
  445.7 15.8 all-gather.1
  472.9 44.5 reduce-scatter.1
where the time goes:
time: 528 us; the launch traced here: 526 us
  local copies, waits for them, and re-layouts  153 us (29%)
  matrix products  132 us (25%)
  blocking collectives  97.5 us (18%)
  waiting for transfers between devices  67.9 us (13%)
  other arithmetic  30.5 us (6%)
  loops' own time  21 us (4%)
  between operations  13.6 us (3%)
  starting transfers between devices  10.9 us (2%)
    gather x1, local copies, waits for them, and re-layouts, local(): gathered = jnp.take(flat_table, rows_in, axis=0)  115 us
    all_to_all x1, blocking collectives, local(): lax.all_to_all(partial_value, 'gx', split_axis=0, concat_axis=0, tiled=True)  97.5 us
    dot_general x32, matrix products, fill_owner(): return jnp.dot(marks, carried_one, preferred_element_type=jnp.float32)  83.8 us
    reduce_scatter x1, waiting for transfers between devices, local(): lax.psum_scatter(jnp.dot(hidden_rows, top_out, preferred_element_type=jnp...  44.8 us
    dot_general x8, matrix products, pool_source(): jnp.einsum('tbs,tsd->tbd', selector, rows_one, precision=lax.Precision.HI...  37.4 us
    dynamic_slice x32, local copies, waits for them, and re-layouts, fill_table(): return lax.map(fill_owner, jnp.arange(owners, dtype=jnp.int32))  20.9 us
    another operation x4, loops' own time, fill_table(): return lax.map(fill_owner, jnp.arange(owners, dtype=jnp.int32))  20.7 us
    all_gather x1, waiting for transfers between devices, local(): lax.all_gather(features, 'gy', axis=0, tiled=True)  15.7 us
  transfers between devices with their start and end apart: 4, of which 3 were waited for; matrix products, arithmetic and copies ran while one was open for 24% of the time, Pallas kernels for 0%

commit v1 on v0

v1 whole, which is shorter than its diff:
```python
import functools
import jax
import jax.numpy as jnp
from jax import lax
from jax.experimental import pallas as pl
from jax.experimental.pallas import tpu as pltpu
from jax.sharding import PartitionSpec as P

UNROLL = 4
CHAINS = 4
BIG = 2**31 - 1


def log2(n):
    return n.bit_length() - 1


def sort_kernel(rows_dev, owner_ref, row_ref, bag_ref, out_ref):
    tables, bag_size, samples = owner_ref.shape
    owner = owner_ref[...]
    slot = lax.broadcasted_iota(jnp.int32, owner.shape, 1)
    sample = lax.broadcasted_iota(jnp.int32, owner.shape, 2)
    live = slot < bag_ref[...]
    key = jnp.where(live, (owner * samples + sample) * rows_dev + row_ref[...], BIG)
    count = bag_size * samples
    groups = count // 1024
    parts = []
    for t in range(tables):
        for c in range(samples // 128):
            for r in range(bag_size // 8):
                parts.append(key[t, r * 8 : r * 8 + 8, c * 128 : c * 128 + 128])
    lane = lax.broadcasted_iota(jnp.int32, (8, 128), 1)
    sub = lax.broadcasted_iota(jnp.int32, (8, 128), 0)
    place = sub * 128 + lane
    bits = log2(count)
    for k in range(1, bits + 1):
        for j in range(k - 1, -1, -1):
            d = 1 << j
            new = [None] * len(parts)
            for v in range(len(parts)):
                g = v % groups
                if d >= 1024:
                    gd = d // 1024
                    if g & gd:
                        continue
                    w = v + gd
                    low = jnp.minimum(parts[v], parts[w])
                    high = jnp.maximum(parts[v], parts[w])
                    up = ((g * 1024) >> k) & 1 == 0
                    new[v], new[w] = (low, high) if up else (high, low)
                    continue
                x = parts[v]
                if d < 128:
                    a, b = pltpu.roll(x, 128 - d, 1), pltpu.roll(x, d, 1)
                else:
                    s = d // 128
                    a, b = pltpu.roll(x, 8 - s, 0), pltpu.roll(x, s, 0)
                first = (place & d) == 0
                other = jnp.where(first, a, b)
                if (1 << k) >= 1024:
                    up = ((g * 1024) >> k) & 1 == 0
                    take_low = first if up else jnp.logical_not(first)
                else:
                    take_low = ((place >> k) ^ (place >> j)) & 1 == 0
                new[v] = jnp.where(take_low, jnp.minimum(x, other), jnp.maximum(x, other))
            parts = new
    for v in range(len(parts)):
        out_ref[v * 8 : v * 8 + 8, :] = parts[v]


def pool_kernel(samples, count, window, lo_ref, n_ref, keys_ref, table_ref, out_ref, tab, acc, smem, tsem, ksem):
    tables, rows_dev, emb = table_ref.shape
    sources = out_ref.shape[0]
    mask = rows_dev - 1
    shift = log2(rows_dev)
    segs = sources * tables

    def table_copy(t):
        return pltpu.make_async_copy(table_ref.at[t], tab.at[t % 2], tsem.at[t % 2])

    def key_copy(s, t, slot):
        start = lo_ref[s, t] // 1024 * 1024
        start = jnp.minimum(start, count - window)
        src = keys_ref.at[pl.ds(pl.multiple_of((s * tables + t) * count + start, 1024), window)]
        dst = smem.at[pl.ds(slot * window, window)]
        return pltpu.make_async_copy(src, dst, ksem.at[slot])

    steps = [(t, g) for t in range(tables) for g in range(sources // CHAINS)]

    def start_keys(index):
        t, g = steps[index]
        for j in range(CHAINS):
            key_copy(g * CHAINS + j, t, index % 2 * CHAINS + j).start()

    table_copy(0).start()
    start_keys(0)
    for index, (t, g) in enumerate(steps):
        if g == 0:
            if t + 1 < tables:
                table_copy(t + 1).start()
            table_copy(t).wait()
        if index + 1 < len(steps):
            start_keys(index + 1)
        acc[...] = jnp.zeros_like(acc)
        bases, longest = [], 0
        for j in range(CHAINS):
            s = g * CHAINS + j
            slot = index % 2 * CHAINS + j
            key_copy(s, t, slot).wait()
            start = jnp.minimum(lo_ref[s, t] // 1024 * 1024, count - window)
            bases.append(slot * window + lo_ref[s, t] - start)
            longest = jnp.maximum(longest, n_ref[s, t])
        limits = [slot_end for slot_end in range(CHAINS)]
        del limits

        def body(i, carry):
            prevs, runs = list(carry[0]), list(carry[1])
            for u in range(UNROLL):
                for j in range(CHAINS):
                    at = jnp.minimum(bases[j] + i * UNROLL + u, (index % 2 * CHAINS + j + 1) * window - 1)
                    code = smem[at]
                    valid = i * UNROLL + u < n_ref[g * CHAINS + j, t]
                    bag = jnp.where(valid, (code >> shift) & (samples - 1), samples)
                    row = code & mask
                    got = tab[t % 2, pl.ds(row, 1), :]
                    runs[j] = jnp.where(bag == prevs[j], runs[j], 0.0) + got
                    acc[pl.ds(j * (samples + 8) + bag, 1), :] = runs[j]
                    prevs[j] = bag
            return tuple(prevs), tuple(runs)

        init = (
            tuple(jnp.int32(-1) for _ in range(CHAINS)),
            tuple(jnp.zeros((1, emb), jnp.float32) for _ in range(CHAINS)),
        )
        lax.fori_loop(0, (longest + UNROLL - 1) // UNROLL, body, init)
        for j in range(CHAINS):
            out_ref[g * CHAINS + j, :, t * emb : (t + 1) * emb] = acc[
                j * (samples + 8) : j * (samples + 8) + samples, :
            ].astype(out_ref.dtype)


def local(table, lookup_owner, lookup_row, bag_length, top_in, top_bias, top_out):
    owners = lax.axis_size("gx")
    me = lax.axis_index("gx")
    tables, samples, bag_size = lookup_row.shape
    rows_dev = table.shape[1]
    emb = table.shape[2]
    count = samples * bag_size
    cap = 2 * count // owners
    window = min(count, -(-cap // 1024) * 1024 + 1024)

    keys = pl.pallas_call(
        functools.partial(sort_kernel, rows_dev),
        out_shape=jax.ShapeDtypeStruct((tables * count // 128, 128), jnp.int32),
        name="sort_keys",
    )(
        jnp.transpose(lookup_owner[..., 0], (0, 2, 1)),
        jnp.transpose(lookup_row, (0, 2, 1)),
        bag_length[:, None, :],
    )
    all_keys = lax.all_gather(keys, "gx", axis=0, tiled=True)
    span = samples * rows_dev
    segs = all_keys.reshape(owners, tables, count)
    lo = jnp.sum((segs < me * span).astype(jnp.int32), axis=2)
    hi = jnp.sum((segs < (me + 1) * span).astype(jnp.int32), axis=2)
    partial = pl.pallas_call(
        functools.partial(pool_kernel, samples, count, window),
        out_shape=jax.ShapeDtypeStruct((owners, samples, tables * emb), jnp.bfloat16),
        in_specs=[
            pl.BlockSpec(memory_space=pltpu.SMEM),
            pl.BlockSpec(memory_space=pltpu.SMEM),
            pl.BlockSpec(memory_space=pl.ANY),
            pl.BlockSpec(memory_space=pl.ANY),
        ],
        scratch_shapes=[
            pltpu.VMEM((2, rows_dev, emb), jnp.float32),
            pltpu.VMEM((CHAINS * (samples + 8), emb), jnp.float32),
            pltpu.SMEM((2 * CHAINS * window,), jnp.int32),
            pltpu.SemaphoreType.DMA((2,)),
            pltpu.SemaphoreType.DMA((2 * CHAINS,)),
        ],
        name="pool",
    )(lo, hi - lo, all_keys.reshape(-1), table)
    answer = lax.all_to_all(partial, "gx", split_axis=0, concat_axis=0, tiled=True)
    features = jnp.sum(answer.astype(jnp.float32), axis=0).astype(jnp.bfloat16)
    pre_act = (
        jnp.dot(
            lax.all_gather(features, "gy", axis=0, tiled=True),
            top_in,
            preferred_element_type=jnp.float32,
        )
        + top_bias
    )
    hidden_rows = jnp.maximum(pre_act, 0.0).astype(jnp.bfloat16)
    return lax.psum_scatter(
        jnp.dot(hidden_rows, top_out, preferred_element_type=jnp.float32).astype(jnp.bfloat16),
        "gy",
        scatter_dimension=0,
        tiled=True,
    )


def solution(mesh):
    return jax.shard_map(
        local,
        mesh=mesh,
        in_specs=(
            P(None, "gx", None),
            P(None, ("gx", "gy"), None, None),
            P(None, ("gx", "gy"), None),
            P(None, ("gx", "gy")),
            P(None, "gy"),
            P("gy"),
            P("gy", None),
        ),
        out_specs=P(("gx", "gy"), None),
        check_vma=False,
    )
```

time: 528 us -> 251 us (0.48)
  local copies, waits for them, and re-layouts: 153 us -> 6.14 us
  matrix products: 132 us -> 10.5 us
  Pallas kernels: 0 us -> 73.8 us
  other arithmetic: 30.5 us -> 5.89 us
  loops' own time: 21 us -> 0 us
  waiting for transfers between devices: 67.9 us -> 49.1 us
  starting transfers between devices: 10.9 us -> 0.04 us
  blocking collectives: 97.5 us -> 91.2 us
    dot_general x40 -> x0, matrix products: 121 us -> none  [the longest x32 83.8 us: fill_owner(): return jnp.dot(marks, carried_one, preferred_element_type=jnp.float32)]
    gather x1 -> x0, local copies, waits for them, and re-layouts: 115 us -> none  [local(): gathered = jnp.take(flat_table, rows_in, axis=0)]
    pallas_call x0 -> x2, Pallas kernels: none -> 73.8 us  [the longest x1 67.8 us: local(): pl.pallas_call(functools.partial(pool_kernel, samples, count, window), ou...]
    all_to_all x1, blocking collectives: 97.5 us -> 58 us  [local(): lax.all_to_all(partial, 'gx', split_axis=0, concat_axis=0, tiled=True)]
    all_gather x0 -> x1, blocking collectives: none -> 33.2 us  [local(): all_keys = lax.all_gather(keys, 'gx', axis=0, tiled=True)]
    dynamic_slice x36 -> x0, local copies, waits for them, and re-layouts: 24.3 us -> none  [the longest x32 20.9 us: fill_table(): return lax.map(fill_owner, jnp.arange(owners, dtype=jnp.int32))]
    another operation x6 -> x0, loops' own time: 21 us -> none  [the longest x4 20.7 us: fill_table(): return lax.map(fill_owner, jnp.arange(owners, dtype=jnp.int32))]
    reduce_scatter x1, waiting for transfers between devices: 44.8 us -> 31.3 us  [local(): lax.psum_scatter(jnp.dot(hidden_rows, top_out, preferred_element_type=jnp...]
  transfers between devices with their start and end apart: 4 -> 2, of which waited for: 3 -> 2; matrix products, arithmetic and copies ran while one was open for 24% -> 0% of each run, Pallas kernels for 0% -> 0%
where the time goes in v1:
time: 251 us; the launch traced here: 250 us
  blocking collectives  91.2 us (36%)
  Pallas kernels  73.8 us (29%)
  waiting for transfers between devices  49.1 us (20%)
  between operations  13.4 us (5%)
  matrix products  10.5 us (4%)
  local copies, waits for them, and re-layouts  6.14 us (2%)
  other arithmetic  5.89 us (2%)
    pallas_call x1, Pallas kernels, local(): pl.pallas_call(functools.partial(pool_kernel, samples, count, window), ou...  67.8 us
    all_to_all x1, blocking collectives, local(): lax.all_to_all(partial, 'gx', split_axis=0, concat_axis=0, tiled=True)  58 us
    all_gather x1, blocking collectives, local(): all_keys = lax.all_gather(keys, 'gx', axis=0, tiled=True)  33.2 us
    reduce_scatter x1, waiting for transfers between devices, local(): lax.psum_scatter(jnp.dot(hidden_rows, top_out, preferred_element_type=jnp...  31.3 us
    all_gather x1, waiting for transfers between devices, local(): lax.all_gather(features, 'gy', axis=0, tiled=True)  17.7 us
    dot_general x1, matrix products, local(): jnp.dot(hidden_rows, top_out, preferred_element_type=jnp.float32)  10.5 us
    pallas_call x1, Pallas kernels, local(): pl.pallas_call(functools.partial(sort_kernel, rows_dev), out_shape=jax.Sh...  6 us
  transfers between devices with their start and end apart: 2, of which 2 were waited for; matrix products, arithmetic and copies ran while one was open for 0% of the time, Pallas kernels for 0%

profile of v1, /device:TPU:0, one launch (start us, length us, event | category | flops | bytes accessed | tf_op | source)
XLA Modules:
  0.0 250.0 jit_solution(4126321635162563034)
XLA Ops:
  6.5 0.0 copy-start
  6.5 0.0 all-gather.2.cloned.1.call-start
  6.5 1.4 broadcast_in_dim.4.bag_ref
  8.0 1.5 copy.10
  9.4 6.0 %sort_keys.1 = s32[128,128]{1,0:T(8,128)} custom-call(s32[4,16,256]{2,1,0:T(8,128)} %bitcast.11, s32[4,16,256]{2,1,0:T(8,128)} %bitcast.12, s32[4,1,256]{2,1,0:T(1,128)} %broadcast_in_dim.4.bag_ref), custom_call_target="tpu_custom_call" | custom-call | tf_op jit(solution)/shard_map/sort_keys/pallas_call | solution.py:152
  15.4 33.2 %all_gather.6 = s32[1024,128]{1,0:T(8,128)S(1)} all-gather(s32[128,128]{1,0:T(8,128)} %sort_keys.1), channel_id=1, replica_groups=mesh['gx'=8,'gy'=4] {'gx'}, dimensions={0}, use_global_device_ids=true | all-gather | bytes 589824 | tf_op jit(solution)/shard_map/all_gather | solution.py:161
  48.7 1.1 compare_convert_fusion
  49.8 1.2 reshape.15
  51.0 2.0 reshape.14
  53.0 0.2 reduce_sum.31
  53.3 1.3 reduce_sum.30.lo_ref
  54.6 0.0 copy-start.2
  54.6 0.6 sub.3.n_ref
  55.2 0.0 copy-done.1
  55.2 67.8 %pool.1 = bf16[8,256,512]{2,1,0:T(8,128)(2,1)} custom-call(s32[8,4]{1,0:T(8,128)} %copy-done.2, s32[8,4]{1,0:T(8,128)} %sub.3.n_ref, s32[131072]{0:T(1024)} %bitcast.10, f32[4,8192,128]{2,1,0:T(8,128)} %table_ref.1), custom_call_target="tpu_custom_call" | custom-call | tf_op jit(solution)/shard_map/pool/pallas_call | solution.py:166
  122.9 0.0 copy-start.3
  122.9 58.0 %all_to_all.5 = bf16[8,256,512]{2,1,0:T(8,128)(2,1)} all-to-all(bf16[8,256,512]{2,1,0:T(8,128)(2,1)} %pool.1), channel_id=1, replica_groups=mesh['gx'=8,'gy'=4] {'gx'}, dimensions={0} | all-to-all | bytes 4194304 | tf_op jit(solution)/shard_map/all_to_all | solution.py:184
  180.9 2.7 %reduce_sum.32 = bf16[256,512]{1,0:T(8,128)(2,1)} reduce(bf16[8,256,512]{2,1,0:T(8,128)(2,1)} %all_to_all.5, bf16[]{:T(256)} %constant.15.clone.1), dimensions={0}, to_apply=%region_2.0 | reduce | flops 917504 | bytes 2359298 | tf_op jit(solution)/shard_map/reduce_sum | solution.py:185
  183.6 0.0 all-gather.2.cloned.1.call-update
  183.6 0.0 reduce-scatter.2.cloned.1.call-start
  183.6 17.7 %all-gather.2.cloned.1.call-done = bf16[1024,512]{1,0:T(8,128)(2,1)} async-done(((bf16[256,512]{1,0:T(8,128)(2,1)}), bf16[1024,512]{1,0:T(8,128)(2,1)}) %all-gather.2.cloned.1.call-update) | async-done | bytes 1048592 | tf_op jit(solution)/shard_map/all_gather | solution.py:188
  201.3 10.5 %fusion.3 = bf16[1024,1024]{1,0:T(8,128)(2,1)} fusion(bf16[2048,1024]{1,0:T(8,128)(2,1)} %param.13, f32[2048]{0:T(1024)S(1)} %copy-done.3, bf16[1024,512]{1,0:T(8,128)(2,1)} %all-gather.2.cloned.1.call-done, bf16[512,2048]{1,0:T(8,128)(2,1)S(1)} %copy-done), kind=kOutput, calls=%fused_computation.4 | convolution fusion | flops 6449790976 | bytes 9445376 | tf_op jit(solution)/shard_map/dot_general | solution.py:196
  211.9 0.0 reduce-scatter.2.cloned.1.call-update
  211.9 31.3 %reduce-scatter.2.cloned.1.call-done = bf16[256,1024]{1,0:T(8,128)(2,1)} async-done(((bf16[1024,1024]{1,0:T(8,128)(2,1)}), bf16[256,1024]{1,0:T(8,128)(2,1)}) %reduce-scatter.2.cloned.1.call-update) | async-done | bytes 524304 | tf_op jit(solution)/shard_map/reduce_scatter | solution.py:195
  (4 shorter events, 0.0 us)
Async XLA Ops:
  6.5 194.8 %copy-start = (bf16[512,2048]{1,0:T(8,128)(2,1)S(1)}, bf16[512,2048]{1,0:T(8,128)(2,1)}, u32[]{:S(2)}) copy-start(bf16[512,2048]{1,0:T(8,128)(2,1)} %param.11) | copy-start | bytes 6291460
  6.5 194.8 %all-gather.2.cloned.1.call-start = ((), (), s32[]{:S(2)}) async-start(), calls=%async_computation.2 | async-start | bytes 1310720 | tf_op jit(solution)/shard_map/all_gather | solution.py:188
  48.7 6.5 %copy-start.1 = (s32[1024,128]{1,0:T(8,128)}, s32[1024,128]{1,0:T(8,128)S(1)}, u32[]{:S(2)}) copy-start(s32[1024,128]{1,0:T(8,128)S(1)} %all_gather.6) | copy-start | bytes 1572868
  54.6 0.6 copy-start.2
  122.9 78.4 %copy-start.3 = (f32[2048]{0:T(1024)S(1)}, f32[2048]{0:T(1024)}, u32[]{:S(2)}) copy-start(f32[2048]{0:T(1024)} %param.12) | copy-start | bytes 24580
  183.6 59.6 %reduce-scatter.2.cloned.1.call-start = ((), (), s32[]{:S(2)}) async-start(), calls=%async_computation.3 | async-start | bytes 2621440 | tf_op jit(solution)/shard_map/reduce_scatter | solution.py:195
Sparse Core Ops, SparseCore 0:
  183.7 17.5 all-gather.1
  212.0 31.1 reduce-scatter.1
